TPU v7x, 32 devices: a whole 2x2x4 slice. The times are simulated.
32 devices in a mesh: dp: 16 (over z, y, x), mp: 2 (over core).
Axes of the slice: x: 2, y: 2, z: 4, core: 2. Of those that a mesh axis runs over, the one named last changes fastest.
Arguments:
- q_new: bfloat16 [32, 8, 256], P('dp', 'mp'), may hold values from -6 to 6
- k_new: bfloat16 [32, 8, 256], P('dp', 'mp'), may hold values from -6 to 6
- v_new: bfloat16 [32, 8, 256], P('dp', 'mp'), may hold values from -6 to 6
- k_cache: bfloat16 [32, 8, 1024, 256], P('dp', 'mp'), may hold values from -6 to 6
- v_cache: bfloat16 [32, 8, 1024, 256], P('dp', 'mp'), may hold values from -6 to 6
- lengths: int32 [32], P('dp'), may hold values from 1 to 1024
- memory: float32 [32, 8, 256, 256], P('dp', 'mp'), may hold values from -6 to 6
- norm_z: float32 [32, 8, 256], P('dp', 'mp'), may hold values from 0.01 to 0.1
- beta: float32 [8], P('mp'), may hold values from -2 to 2
- out_weight: bfloat16 [2048, 2048], P(None, 'mp'), may hold values from -0.125 to 0.125
- residual_in: bfloat16 [32, 2048], P('dp', 'mp'), may hold values from -45 to 45
- final_gain: float32 [2048], replicated, may hold values from 0.5 to 1.5
- embedding: bfloat16 [8192, 2048], P(('dp', 'mp')), may hold values from -0.9943689 to 0.9943689
Outputs:
- hidden_out: bfloat16 [32, 2048], P('dp', 'mp')
- log_probs: float32 [32, 8192], P(None, ('dp', 'mp'))
All inputs are finite; a program needn't handle non-finite values.
Results may differ from a plain program's by a relative error of at most 0.0033.
Values may be sent and summed in bfloat16 or wider, within the bound.
A program may use at most 64 MiB of HBM per device.

v0:
```python
import math

import jax
import jax.numpy as jnp
from jax import lax
from jax.sharding import PartitionSpec as P

D = 2048
HD = 256


epsilon = 1e-06


def body(
    q_new,
    k_new,
    v_new,
    k_cache,
    v_cache,
    lengths,
    memory,
    norm_z,
    beta,
    out_weight,
    residual_in,
    final_gain,
    embedding,
):
    floating = jnp.float32
    scaling = 1.0 / math.sqrt(HD)
    batch_here = q_new.shape[0]
    scores = jnp.einsum("bhd,bhld->bhl", q_new, k_cache, preferred_element_type=floating)
    scores = 50.0 * jnp.tanh(scores * scaling / 50.0)
    own_score = jnp.sum(q_new.astype(floating) * k_new.astype(floating), axis=-1)
    own_score = 50.0 * jnp.tanh(own_score * scaling / 50.0)
    slot_index = jnp.arange(k_cache.shape[2], dtype=jnp.int32)
    live = slot_index[None, None, :] < lengths[:, None, None]
    weights = jnp.where(live, jnp.exp(scores), 0.0)
    self_token_weight = jnp.exp(own_score)
    summed = jnp.sum(weights, axis=-1) + self_token_weight
    weights_bf = weights.astype(jnp.bfloat16)
    own_bf = self_token_weight.astype(jnp.bfloat16).astype(floating)
    local = jnp.einsum("bhl,bhld->bhd", weights_bf, v_cache, preferred_element_type=floating)
    local = (local + own_bf[..., None] * v_new.astype(floating)) / summed[..., None]
    raised_features = jax.nn.elu(q_new.astype(floating)) + 1.0
    memory_retrieval = jnp.einsum(
        "bhk,bhkv->bhv", raised_features, memory, precision=lax.Precision.HIGHEST
    )
    memory_retrieval = memory_retrieval / jnp.sum(raised_features * norm_z, axis=-1)[..., None]
    gate = jax.nn.sigmoid(beta)[None, :, None]
    head_out = (gate * memory_retrieval + (1.0 - gate) * local).astype(jnp.bfloat16)
    head_flat = head_out.reshape(batch_here, -1)
    feature_width = out_weight.shape[1]
    projected = jnp.dot(
        lax.all_gather(head_flat, "mp", axis=1, tiled=True),
        out_weight,
        preferred_element_type=floating,
    )
    hidden_out = (residual_in.astype(floating) + projected).astype(jnp.bfloat16)
    group_count = lax.axis_size("mp")
    gathered = lax.all_gather(hidden_out[None], ("dp", "mp"), axis=0, tiled=True)
    grouped = gathered.reshape(-1, group_count, batch_here, feature_width)
    grouped_f = grouped.astype(floating)
    squared_values_global = jnp.sum(grouped_f * grouped_f, axis=(1, 3))
    gain_blocks = final_gain.reshape(group_count, 1, feature_width)
    normed = (
        grouped_f
        * lax.rsqrt(squared_values_global / D + epsilon)[:, None, :, None]
        * gain_blocks[None]
    ).astype(jnp.bfloat16)
    vocab_here = embedding.shape[0]
    embedding_tiles = embedding.reshape(vocab_here, group_count, feature_width)
    unscaled = jnp.einsum("pmbd,vmd->pbv", normed, embedding_tiles, preferred_element_type=floating)
    logits = 30.0 * jnp.tanh(unscaled.reshape(-1, vocab_here) / 30.0)
    exponent_sum_total = lax.psum(jnp.sum(jnp.exp(logits), axis=1), ("dp", "mp"))
    return (hidden_out, logits - jnp.log(exponent_sum_total)[:, None])


def solution(mesh):
    in_specs = (
        P("dp", "mp", None),
        P("dp", "mp", None),
        P("dp", "mp", None),
        P("dp", "mp", None, None),
        P("dp", "mp", None, None),
        P("dp"),
        P("dp", "mp", None, None),
        P("dp", "mp", None),
        P("mp"),
        P(None, "mp"),
        P("dp", "mp"),
        P(),
        P(("dp", "mp"), None),
    )
    out_specs = (P("dp", "mp"), P(None, ("dp", "mp")))
    return jax.shard_map(body, mesh=mesh, in_specs=in_specs, out_specs=out_specs, check_vma=False)
```

profile of v0, /device:TPU:0, one launch (start us, length us, event | category | flops | bytes accessed | tf_op | source)
XLA Modules:
  0.0 94.3 jit_solution(5994447489698464736)
XLA Ops:
  0.6 0.0 copy-start
  0.6 0.8 broadcast_subtract_fusion.1
  1.5 0.7 iota_compare_fusion
  2.2 0.7 mul.86
  2.9 0.0 copy-start.1
  2.9 0.9 %fusion.19 = (f32[2,4]{1,0:T(2,128)S(1)}, f32[2,4,256,1]{2,1,0,3:T(4,128)S(1)}) fusion(bf16[2,4,256]{2,1,0:T(4,128)(2,1)} %param.13, bf16[2,4,256]{2,1,0:T(4,128)(2,1)} %param.14), kind=kLoop, calls=%fused_computation.30 | loop fusion | flops 16376 | bytes 16416 | tf_op jit(solution)/shard_map/reduce_sum | solution.py:35
  3.8 0.0 copy-done
  3.8 1.1 %fusion.25 = f32[2,4,1,256]{3,2,1,0:T(1,128)S(1)} fusion(f32[2,4,256,256]{3,2,1,0:T(8,128)S(1)} %copy-done, f32[2,4,256,1]{2,1,0,3:T(4,128)S(1)} %get-tuple-element.7), kind=kOutput, calls=%fused_computation.38 | convolution fusion | flops 6291456 | bytes 2113536 | tf_op jit(solution)/shard_map/bhk,bhkv->bhv/dot_general | solution.py:47
  4.9 0.0 copy-start.3
  4.9 0.0 copy-start.7
  5.0 0.0 copy-start.8
  5.0 0.0 copy-start.2
  5.0 0.0 copy-start.5
  5.0 3.5 %fusion.23 = f32[2,4,1,1024]{3,2,1,0:T(1,128)S(1)} fusion(bf16[2,4,1024,256]{3,2,1,0:T(8,128)(2,1)} %param.16, bf16[2,4,256,1]{2,1,0,3:T(4,128)(2,1)} %bitcast.60), kind=kOutput, calls=%fused_computation.36 | convolution fusion | flops 4194304 | bytes 4231168 | tf_op jit(solution)/shard_map/bhd,bhld->bhl/dot_general | solution.py:33
  8.5 0.1 fusion.27
  8.7 0.0 copy-done.1
  8.7 0.0 copy-start.6
  8.7 0.7 fusion.17
  9.3 0.0 copy-done.3
  9.3 0.0 copy-done.7
  9.3 0.0 copy-done.8
  9.3 0.1 fusion.9
  9.5 2.0 %all_gather.6 = bf16[2,2048]{1,0:T(2,128)(2,1)S(1)} all-gather(bf16[2,1024]{1,0:T(2,128)(2,1)S(1)} %bitcast.61), channel_id=1, replica_groups=mesh['dp'=16,'mp'=2] {'mp'}, dimensions={1}, use_global_device_ids=true | all-gather | bytes 12288 | tf_op jit(solution)/shard_map/all_gather | solution.py:56
  11.4 0.0 copy-done.2
  11.4 0.0 copy-done.5
  11.4 0.7 fusion.7
  12.1 0.0 copy-start.4
  12.1 43.5 %all-gather.1 = bf16[32,2,1024]{2,1,0:T(2,128)(2,1)S(1)} all-gather(bf16[1,2,1024]{2,1,0:T(2,128)(2,1)S(1)} %bitcast.62), channel_id=2, replica_groups=mesh['dp'=16,'mp'=2] {'dp','mp'}, dimensions={0}, use_global_device_ids=true | all-gather | bytes 135168 | tf_op jit(solution)/shard_map/all_gather | solution.py:62
  55.5 0.2 multiply_reduce_fusion
  55.8 0.2 fusion.12
  56.0 0.1 copy.25
  56.1 0.1 dot_general.24
  56.2 0.0 copy-done.6
  56.2 0.5 exponential_reduce_fusion
  56.7 36.8 %psum.7 = f32[32]{0:T(128)S(1)} all-reduce(f32[32]{0:T(128)S(1)} %get-tuple-element.10), channel_id=1, replica_groups=mesh['dp'=16,'mp'=2] {'dp','mp'}, use_global_device_ids=true, to_apply=%region_6.7 | all-reduce | flops 32 | bytes 256 | tf_op jit(solution)/shard_map/psum | solution.py:76
  93.6 0.7 broadcast_subtract_fusion
  94.3 0.0 copy-done.4
  (5 shorter events, 0.1 us)
Async XLA Ops:
  0.6 3.2 %copy-start = (f32[2,4,256,256]{3,2,1,0:T(8,128)S(1)}, f32[2,4,256,256]{3,2,1,0:T(8,128)}, u32[]{:S(2)}) copy-start(f32[2,4,256,256]{3,2,1,0:T(8,128)} %param.19) | copy-start | bytes 6291460
  2.9 5.8 %copy-start.1 = (bf16[2,4,1024,256]{3,2,1,0:T(8,128)(2,1)S(1)}, bf16[2,4,1024,256]{3,2,1,0:T(8,128)(2,1)}, u32[]{:S(2)}) copy-start(bf16[2,4,1024,256]{3,2,1,0:T(8,128)(2,1)} %param.17) | copy-start | bytes 12582916
  4.9 4.4 %copy-start.3 = (bf16[2,4,256]{2,1,0:T(4,128)(2,1)S(1)}, bf16[2,4,256]{2,1,0:T(4,128)(2,1)}, u32[]{:S(2)}) copy-start(bf16[2,4,256]{2,1,0:T(4,128)(2,1)} %param.13) | copy-start | bytes 12292
  4.9 4.4 %copy-start.7 = (f32[2,4,256]{2,1,0:T(4,128)S(1)}, f32[2,4,256]{2,1,0:T(4,128)}, u32[]{:S(2)}) copy-start(f32[2,4,256]{2,1,0:T(4,128)} %param.20) | copy-start | bytes 24580
  5.0 4.4 %copy-start.8 = (bf16[2,4,256]{2,1,0:T(4,128)(2,1)S(1)}, bf16[2,4,256]{2,1,0:T(4,128)(2,1)}, u32[]{:S(2)}) copy-start(bf16[2,4,256]{2,1,0:T(4,128)(2,1)} %param.15) | copy-start | bytes 12292
  5.0 6.5 %copy-start.2 = (bf16[2048,1024]{1,0:T(8,128)(2,1)S(1)}, bf16[2048,1024]{1,0:T(8,128)(2,1)}, u32[]{:S(2)}) copy-start(bf16[2048,1024]{1,0:T(8,128)(2,1)} %param.22) | copy-start | bytes 12582916
  5.0 6.5 %copy-start.5 = (bf16[2,1024]{1,0:T(2,128)(2,1)S(1)}, bf16[2,1024]{1,0:T(2,128)(2,1)}, u32[]{:S(2)}) copy-start(bf16[2,1024]{1,0:T(2,128)(2,1)} %param.23) | copy-start | bytes 12292
  8.7 47.5 %copy-start.6 = (bf16[256,2048]{1,0:T(8,128)(2,1)S(1)}, bf16[256,2048]{1,0:T(8,128)(2,1)}, u32[]{:S(2)}) copy-start(bf16[256,2048]{1,0:T(8,128)(2,1)} %param.25) | copy-start | bytes 3145732
  12.1 82.2 %copy-start.4 = (bf16[2,1024]{1,0:T(2,128)(2,1)}, bf16[2,1024]{1,0:T(2,128)(2,1)S(1)}, u32[]{:S(2)}) copy-start(bf16[2,1024]{1,0:T(2,128)(2,1)S(1)} %fusion.7) | copy-start | bytes 12292
where the time goes:
time: 95.2 us; the launch traced here: 94.3 us
  blocking collectives  82.3 us (86%)
  matrix products  6.47 us (7%)
  other arithmetic  3.88 us (4%)
    all_gather x1, blocking collectives, body(): lax.all_gather(hidden_out[None], ('dp', 'mp'), axis=0, tiled=True)  43.5 us
    psum x1, blocking collectives, body(): lax.psum(jnp.sum(jnp.exp(logits), axis=1), ('dp', 'mp'))  36.8 us
    dot_general x1, matrix products, body(): jnp.einsum('bhd,bhld->bhl', q_new, k_cache, preferred_element_type=floating)  3.53 us
    all_gather x1, blocking collectives, body(): lax.all_gather(head_flat, 'mp', axis=1, tiled=True)  1.96 us

commit v1 on v0

v1 whole, which is shorter than its diff:
```python
import functools
import math

import jax
import jax.numpy as jnp
from jax import lax
from jax.experimental import pallas as pl
from jax.experimental.pallas import tpu as pltpu
from jax.sharding import PartitionSpec as P

MESH = pl.DeviceIdType.MESH
F32 = jnp.float32
BF16 = jnp.bfloat16
LANES = 128
epsilon = 1e-06

NT = (((1,), (1,)), ((), ()))


def up(value, step):
    return -(-value // step) * step


def kernel(
    DP, MP, B, H, HD, L, FW, CP,
    lengths_ref, beta_ref, q_hbm, kn_hbm, vn_hbm, k_hbm, v_hbm, mem_hbm, nz_hbm, w_hbm, res_hbm, gain_hbm, e_hbm,
    hid_ref, out_ref,
    q_in, kn_in, vn_in, nz_in, res, gain, k_vm, v_vm, m_vm, w_vm, e_vm,
    flat, heads, tile, gath, gf, sums,
    small_sem, k_sem, v_sem, m_sem, w_sem, e_sem,
    h_send, h_recv, g_send, g_recv, s_send, s_recv,
):
    dp, mp = lax.axis_index("dp"), lax.axis_index("mp")
    N = DP * MP
    me = dp * MP + mp
    slot = mp * DP + dp
    pairs = [(b, h) for b in range(B) for h in range(H)]
    PP = flat.shape[1]
    C = FW // LANES
    D = MP * FW
    S = DP * B
    HW = H * HD

    small = [
        pltpu.make_async_copy(src, dst, small_sem.at[i])
        for i, (src, dst) in enumerate(
            [(q_hbm, q_in), (kn_hbm, kn_in), (nz_hbm, nz_in), (vn_hbm, vn_in), (res_hbm, res), (gain_hbm, gain)]
        )
    ]
    k_copy = [pltpu.make_async_copy(k_hbm.at[b, h], k_vm.at[i], k_sem.at[i]) for i, (b, h) in enumerate(pairs)]
    v_copy = [pltpu.make_async_copy(v_hbm.at[b, h], v_vm.at[i], v_sem.at[i]) for i, (b, h) in enumerate(pairs)]
    m_copy = [pltpu.make_async_copy(mem_hbm.at[b, h], m_vm.at[i], m_sem.at[i]) for i, (b, h) in enumerate(pairs)]
    w_copy = []
    for i in range(MP):
        rows = pl.ds(pl.multiple_of(lax.rem(mp + i, MP) * HW, HW), HW)
        w_copy.append(pltpu.make_async_copy(w_hbm.at[rows], w_vm.at[rows], w_sem.at[i]))
    e_copy = pltpu.make_async_copy(e_hbm, e_vm, e_sem)
    for copy in small[:4] + k_copy + m_copy + v_copy + small[4:] + w_copy + [e_copy]:
        copy.start()

    barrier = pltpu.get_barrier_semaphore()

    @pl.loop(1, N)
    def _(i):
        p = lax.rem(me + i, N)
        pl.semaphore_signal(barrier, inc=1, device_id=(p // MP, lax.rem(p, MP)), device_id_type=MESH)

    if PP != len(pairs):
        flat[...] = jnp.zeros_like(flat)
    row = lax.broadcasted_iota(jnp.int32, (PP, 1), 0)
    for i, src in enumerate([q_in, kn_in, nz_in, vn_in]):
        small[i].wait()
        for b in range(B):
            flat[i, b * H : (b + 1) * H, :] = src[b].astype(F32)
    q, kn, nz, vn = flat[0], flat[1], flat[2], flat[3]
    qb = q.astype(BF16)
    scaling = 1.0 / math.sqrt(HD)

    own = jnp.exp(50.0 * jnp.tanh(jnp.sum(q * kn, axis=1, keepdims=True) * scaling / 50.0))
    sq = jnp.where(q > 0.0, q, jnp.exp(jnp.minimum(q, 0.0)) - 1.0) + 1.0
    denominator = jnp.sum(sq * nz, axis=1, keepdims=True)
    sq_hi = sq.astype(BF16)
    sq_lo = (sq - sq_hi.astype(F32)).astype(BF16)
    sq_both = jnp.concatenate([sq_hi.astype(F32), sq_lo.astype(F32)], axis=0).astype(BF16)

    scores = jnp.zeros((PP, L), F32)
    for i in range(len(pairs)):
        k_copy[i].wait()
        part = lax.dot_general(qb, k_vm[i], NT, preferred_element_type=F32)
        scores = jnp.where(row == i, part, scores)
    live_count = jnp.zeros((PP, 1), jnp.int32)
    gate = jnp.zeros((PP, 1), F32)
    for i, (b, h) in enumerate(pairs):
        live_count = jnp.where(row == i, lengths_ref[b], live_count)
        gate = jnp.where(row == i, beta_ref[h], gate)
    gate = 1.0 / (1.0 + jnp.exp(-gate))
    weights = jnp.exp(50.0 * jnp.tanh(scores * scaling / 50.0))
    live = lax.broadcasted_iota(jnp.int32, (PP, L), 1) < live_count
    weights = jnp.where(live, weights, 0.0)
    total = jnp.sum(weights, axis=1, keepdims=True) + own
    wb = weights.astype(BF16)

    readout = jnp.zeros((PP, HD), F32)
    for i in range(len(pairs)):
        m_copy[i].wait()
        m = m_vm[i]
        m_hi = m.astype(BF16)
        m_lo = (m - m_hi.astype(F32)).astype(BF16)
        first = jnp.dot(sq_both, m_hi, preferred_element_type=F32)
        second = jnp.dot(sq_hi, m_lo, preferred_element_type=F32)
        readout = jnp.where(row == i, first[:PP] + first[PP:] + second, readout)
    readout = readout / denominator

    local = jnp.zeros((PP, HD), F32)
    for i in range(len(pairs)):
        v_copy[i].wait()
        part = jnp.dot(wb, v_vm[i], preferred_element_type=F32)
        local = jnp.where(row == i, part, local)
    local = (local + own.astype(BF16).astype(F32) * vn) / total
    head_out = gate * readout + (1.0 - gate) * local
    heads[mp] = head_out.astype(BF16)

    pl.semaphore_wait(barrier, N - 1)

    def head_send(i):
        m = lax.rem(mp + i, MP)
        return pltpu.make_async_remote_copy(
            src_ref=heads.at[mp], dst_ref=heads.at[mp],
            send_sem=h_send.at[i], recv_sem=h_recv.at[mp],
            device_id=(dp, m), device_id_type=MESH,
        )

    for i in range(1, MP):
        head_send(i).start()

    small[4].wait()
    small[5].wait()
    turn = lax.rem(row, H)
    acc = None
    for i in range(MP):
        m = lax.rem(mp + i, MP)
        w_copy[i].wait()
        if i:
            pltpu.make_async_copy(heads.at[m], heads.at[m], h_recv.at[m]).wait()
        ho = heads[m].astype(F32)
        lhs = jnp.concatenate([jnp.where(turn == h, ho, 0.0) for h in range(H)], axis=1).astype(BF16)
        part = jnp.dot(lhs, w_vm[pl.ds(pl.multiple_of(m * HW, HW), HW), :], preferred_element_type=F32)
        acc = part if acc is None else acc + part

    res_f = res[...].astype(F32)
    if CP != C:
        tile[...] = jnp.zeros_like(tile)
    hidden = []
    for b in range(B):
        mine = jnp.where((row >= b * H) & (row < (b + 1) * H), acc, 0.0)
        h_b = res_f[b : b + 1] + jnp.sum(mine, axis=0, keepdims=True)
        hidden.append(h_b)
        for c in range(C):
            tile[b * CP + c : b * CP + c + 1, :] = h_b[:, c * LANES : (c + 1) * LANES]
    gath[slot] = tile[...].astype(BF16)

    @pl.loop(1, N)
    def _(i):
        p = lax.rem(me + i, N)
        pltpu.make_async_remote_copy(
            src_ref=gath.at[slot], dst_ref=gath.at[slot], send_sem=g_send, recv_sem=g_recv,
            device_id=(p // MP, lax.rem(p, MP)), device_id_type=MESH,
        ).start()

    hid_ref[...] = jnp.concatenate(hidden, axis=0).astype(BF16)
    e_copy.wait()
    others = gath.at[pl.ds(0, N - 1)]
    pltpu.make_async_copy(others, others, g_recv).wait()

    RP = B * CP
    gf[...] = gath[...].astype(F32).reshape(MP, DP * RP, LANES)
    columns = [gf[m, pl.ds(c, S, stride=CP), :] for m in range(MP) for c in range(C)]
    square = functools.reduce(jnp.add, [x * x for x in columns])
    scale = lax.rsqrt(jnp.sum(square, axis=1, keepdims=True) / D + epsilon)
    normed = [(x * scale * gain[:, j * LANES : (j + 1) * LANES]) for j, x in enumerate(columns)]
    normed = jnp.concatenate(normed, axis=1).astype(BF16)
    logits = lax.dot_general(normed, e_vm[...], NT, preferred_element_type=F32)
    logits = 30.0 * jnp.tanh(logits / 30.0)
    mine = jnp.sum(jnp.exp(logits), axis=1, keepdims=True)
    wide = sums.shape[2]
    diagonal = lax.broadcasted_iota(jnp.int32, (S, wide), 0) == lax.broadcasted_iota(jnp.int32, (S, wide), 1)
    sums[me] = jnp.sum(jnp.where(diagonal, mine, 0.0), axis=0, keepdims=True)

    @pl.loop(1, N)
    def _(i):
        p = lax.rem(me + i, N)
        pltpu.make_async_remote_copy(
            src_ref=sums.at[me], dst_ref=sums.at[me], send_sem=s_send, recv_sem=s_recv,
            device_id=(p // MP, lax.rem(p, MP)), device_id_type=MESH,
        ).start()

    others_s = sums.at[pl.ds(0, N - 1)]
    pltpu.make_async_copy(others_s, others_s, s_recv).wait()
    everything = jnp.sum(sums[...], axis=0)
    log_total = jnp.log(jnp.sum(jnp.where(diagonal, everything, 0.0), axis=1, keepdims=True))
    out_ref[...] = logits - log_total

    for i in range(1, MP):
        head_send(i).wait_send()
    pltpu.make_async_copy(others, others, g_send).wait()
    pltpu.make_async_copy(others_s, others_s, s_send).wait()


def solution(mesh):
    DP, MP = mesh.shape["dp"], mesh.shape["mp"]
    N = DP * MP

    def body(q_new, k_new, v_new, k_cache, v_cache, lengths, memory, norm_z, beta, out_weight, residual_in, final_gain, embedding):
        B, H, L, HD = k_cache.shape
        FW = out_weight.shape[1]
        V, D = embedding.shape
        C = FW // LANES
        CP = up(C, 16 // math.gcd(B, 16))
        pairs, PP = B * H, up(B * H, 8)
        S = DP * B
        dma = pltpu.SemaphoreType.DMA
        anywhere = pl.BlockSpec(memory_space=pl.ANY)
        vmem = pl.BlockSpec(memory_space=pltpu.VMEM)
        smem = pl.BlockSpec(memory_space=pltpu.SMEM)
        return pl.pallas_call(
            functools.partial(kernel, DP, MP, B, H, HD, L, FW, CP),
            out_shape=(jax.ShapeDtypeStruct((B, FW), BF16), jax.ShapeDtypeStruct((S, V), F32)),
            in_specs=[smem] * 2 + [anywhere] * 11,
            out_specs=(vmem, vmem),
            scratch_shapes=[
                pltpu.VMEM((B, H, HD), BF16),
                pltpu.VMEM((B, H, HD), BF16),
                pltpu.VMEM((B, H, HD), BF16),
                pltpu.VMEM((B, H, HD), F32),
                pltpu.VMEM((B, FW), BF16),
                pltpu.VMEM((1, D), F32),
                pltpu.VMEM((pairs, L, HD), BF16),
                pltpu.VMEM((pairs, L, HD), BF16),
                pltpu.VMEM((pairs, HD, HD), F32),
                pltpu.VMEM(out_weight.shape, BF16),
                pltpu.VMEM((V, D), BF16),
                pltpu.VMEM((4, PP, HD), F32),
                pltpu.VMEM((MP, PP, HD), BF16),
                pltpu.VMEM((B * CP, LANES), F32),
                pltpu.VMEM((N, B * CP, LANES), BF16),
                pltpu.VMEM((MP, DP * B * CP, LANES), F32),
                pltpu.VMEM((N, 1, up(S, LANES)), F32),
                dma((6,)),
                dma((pairs,)),
                dma((pairs,)),
                dma((pairs,)),
                dma((MP,)),
                dma,
                dma((MP,)),
                dma((MP,)),
                dma,
                dma,
                dma,
                dma,
            ],
            compiler_params=pltpu.CompilerParams(collective_id=0, has_side_effects=True),
            name="decode_step",
        )(
            lengths, beta, q_new, k_new, v_new, k_cache, v_cache, memory, norm_z, out_weight, residual_in,
            final_gain.reshape(1, D), embedding,
        )

    in_specs = (
        P("dp", "mp", None),
        P("dp", "mp", None),
        P("dp", "mp", None),
        P("dp", "mp", None, None),
        P("dp", "mp", None, None),
        P("dp"),
        P("dp", "mp", None, None),
        P("dp", "mp", None),
        P("mp"),
        P(None, "mp"),
        P("dp", "mp"),
        P(),
        P(("dp", "mp"), None),
    )
    out_specs = (P("dp", "mp"), P(None, ("dp", "mp")))
    return jax.shard_map(body, mesh=mesh, in_specs=in_specs, out_specs=out_specs, check_vma=False)
```

time: 95.2 us -> 28.8 us (0.30)
  blocking collectives: 82.3 us -> 0 us
  Pallas kernels: 0 us -> 25.3 us
  matrix products: 6.47 us -> 0 us
  other arithmetic: 3.88 us -> 0 us
  local copies, waits for them, and re-layouts: 0.91 us -> 2.65 us
    all_gather x2 -> x0, blocking collectives: 45.4 us -> none  [the longest x1 43.5 us: body(): lax.all_gather(hidden_out[None], ('dp', 'mp'), axis=0, tiled=True)]
    psum x1 -> x0, blocking collectives: 36.8 us -> none  [body(): lax.psum(jnp.sum(jnp.exp(logits), axis=1), ('dp', 'mp'))]
    pallas_call x0 -> x1, Pallas kernels: none -> 25.3 us  [body(): pl.pallas_call(functools.partial(kernel, DP, MP, B, H, HD, L, FW, CP), ou...]
    dot_general x5 -> x0, matrix products: 6.47 us -> none  [the longest x1 3.53 us: body(): jnp.einsum('bhd,bhld->bhl', q_new, k_cache, preferred_element_type=floating)]
    unnamed x19 -> x2, local copies, waits for them, and re-layouts: 0.06 us -> 2.65 us
    sub x2 -> x0, other arithmetic: 1.51 us -> none  [the longest x1 0.81 us: body(): 1.0 - gate]
    reduce_sum x4 -> x0, other arithmetic: 1.31 us -> none  [the longest x1 0.94 us: body(): jnp.sum(q_new.astype(floating) * k_new.astype(floating), axis=-1)]
where the time goes in v1:
time: 28.8 us; the launch traced here: 28.6 us
  Pallas kernels  25.3 us (88%)
  local copies, waits for them, and re-layouts  2.65 us (9%)
  between operations  0.64 us (2%)
    pallas_call x1, Pallas kernels, body(): pl.pallas_call(functools.partial(kernel, DP, MP, B, H, HD, L, FW, CP), ou...  25.3 us
    unnamed x2, local copies, waits for them, and re-layouts  2.65 us

profile of v1, /device:TPU:0, one launch (start us, length us, event | category | flops | bytes accessed | tf_op | source)
XLA Modules:
  0.0 28.6 jit_solution(11418193070499221748)
XLA Ops:
  0.6 25.3 %decode_step.1 = (bf16[2,1024]{1,0:T(2,128)(2,1)}, f32[32,256]{1,0:T(8,128)}) custom-call(s32[2]{0:T(128)} %lengths_ref.1, f32[4]{0:T(128)} %beta_ref.1, bf16[2,4,256]{2,1,0:T(4,128)(2,1)} %q_hbm.1, bf16[2,4,256]{2,1,0:T(4,128)(2,1)} %kn_hbm.1, bf16[2,4,256]{2,1,0:T(4,128)(2,1)} %vn_hbm.1, bf16[2,4,1024,256]{3,2,1,0:T(8,128)(2,1)} %k_hbm.1, ...), custom_call_target="tpu_custom_call" | custom-call | tf_op jit(solution)/shard_map/decode_step/pallas_call | solution.py:225
  25.9 1.3 %copy.17 = bf16[2,1024]{1,0:T(2,128)(2,1)} copy(bf16[2,1024]{1,0:T(2,128)(2,1)} %get-tuple-element.4) | data formatting | bytes 8192
  27.2 1.4 %copy.18 = f32[32,256]{1,0:T(8,128)} copy(f32[32,256]{1,0:T(8,128)} %get-tuple-element.5) | data formatting | bytes 65536

commit v2 on v1

--- a/solution.py
+++ b/solution.py
@@ -26,13 +26,11 @@
     lengths_ref, beta_ref, q_hbm, kn_hbm, vn_hbm, k_hbm, v_hbm, mem_hbm, nz_hbm, w_hbm, res_hbm, gain_hbm, e_hbm,
     hid_ref, out_ref,
     q_in, kn_in, vn_in, nz_in, res, gain, k_vm, v_vm, m_vm, w_vm, e_vm,
-    flat, heads, tile, gath, gf, sums,
+    len_sm, beta_sm, flat, heads, tile, gath, gf, sums, parts,
     small_sem, k_sem, v_sem, m_sem, w_sem, e_sem,
-    h_send, h_recv, g_send, g_recv, s_send, s_recv,
+    h_send, h_recv, g_send, g_recv, s_send, s_recv, p_send, p_recv, t_send, t_recv,
 ):
     dp, mp = lax.axis_index("dp"), lax.axis_index("mp")
-    N = DP * MP
-    me = dp * MP + mp
     slot = mp * DP + dp
     pairs = [(b, h) for b in range(B) for h in range(H)]
     PP = flat.shape[1]
@@ -41,10 +39,19 @@
     S = DP * B
     HW = H * HD
 
+    barrier = pltpu.get_barrier_semaphore()
+
+    @pl.loop(1, DP)
+    def _(i):
+        pl.semaphore_signal(barrier, inc=1, device_id=(lax.rem(dp + i, DP), mp), device_id_type=MESH)
+
+    for i in range(1, MP):
+        pl.semaphore_signal(barrier, inc=1, device_id=(dp, lax.rem(mp + i, MP)), device_id_type=MESH)
+
     small = [
         pltpu.make_async_copy(src, dst, small_sem.at[i])
         for i, (src, dst) in enumerate(
-            [(q_hbm, q_in), (kn_hbm, kn_in), (nz_hbm, nz_in), (vn_hbm, vn_in), (res_hbm, res), (gain_hbm, gain)]
+            [(q_hbm, q_in), (kn_hbm, kn_in), (nz_hbm, nz_in), (vn_hbm, vn_in), (res_hbm, res), (gain_hbm, gain), (lengths_ref, len_sm), (beta_ref, beta_sm)]
         )
     ]
     k_copy = [pltpu.make_async_copy(k_hbm.at[b, h], k_vm.at[i], k_sem.at[i]) for i, (b, h) in enumerate(pairs)]
@@ -55,15 +62,8 @@
         rows = pl.ds(pl.multiple_of(lax.rem(mp + i, MP) * HW, HW), HW)
         w_copy.append(pltpu.make_async_copy(w_hbm.at[rows], w_vm.at[rows], w_sem.at[i]))
     e_copy = pltpu.make_async_copy(e_hbm, e_vm, e_sem)
-    for copy in small[:4] + k_copy + m_copy + v_copy + small[4:] + w_copy + [e_copy]:
+    for copy in small[:4] + small[6:] + k_copy + m_copy + v_copy + small[4:6] + w_copy + [e_copy]:
         copy.start()
-
-    barrier = pltpu.get_barrier_semaphore()
-
-    @pl.loop(1, N)
-    def _(i):
-        p = lax.rem(me + i, N)
-        pl.semaphore_signal(barrier, inc=1, device_id=(p // MP, lax.rem(p, MP)), device_id_type=MESH)
 
     if PP != len(pairs):
         flat[...] = jnp.zeros_like(flat)
@@ -88,11 +88,13 @@
         k_copy[i].wait()
         part = lax.dot_general(qb, k_vm[i], NT, preferred_element_type=F32)
         scores = jnp.where(row == i, part, scores)
+    small[6].wait()
+    small[7].wait()
     live_count = jnp.zeros((PP, 1), jnp.int32)
     gate = jnp.zeros((PP, 1), F32)
     for i, (b, h) in enumerate(pairs):
-        live_count = jnp.where(row == i, lengths_ref[b], live_count)
-        gate = jnp.where(row == i, beta_ref[h], gate)
+        live_count = jnp.where(row == i, len_sm[b], live_count)
+        gate = jnp.where(row == i, beta_sm[h], gate)
     gate = 1.0 / (1.0 + jnp.exp(-gate))
     weights = jnp.exp(50.0 * jnp.tanh(scores * scaling / 50.0))
     live = lax.broadcasted_iota(jnp.int32, (PP, L), 1) < live_count
@@ -120,7 +122,7 @@
     head_out = gate * readout + (1.0 - gate) * local
     heads[mp] = head_out.astype(BF16)
 
-    pl.semaphore_wait(barrier, N - 1)
+    pl.semaphore_wait(barrier, DP - 1 + MP - 1)
 
     def head_send(i):
         m = lax.rem(mp + i, MP)
@@ -159,18 +161,32 @@
             tile[b * CP + c : b * CP + c + 1, :] = h_b[:, c * LANES : (c + 1) * LANES]
     gath[slot] = tile[...].astype(BF16)
 
-    @pl.loop(1, N)
+    @pl.loop(1, DP)
     def _(i):
-        p = lax.rem(me + i, N)
         pltpu.make_async_remote_copy(
             src_ref=gath.at[slot], dst_ref=gath.at[slot], send_sem=g_send, recv_sem=g_recv,
-            device_id=(p // MP, lax.rem(p, MP)), device_id_type=MESH,
+            device_id=(lax.rem(dp + i, DP), mp), device_id_type=MESH,
         ).start()
 
     hid_ref[...] = jnp.concatenate(hidden, axis=0).astype(BF16)
     e_copy.wait()
-    others = gath.at[pl.ds(0, N - 1)]
+    others = gath.at[pl.ds(0, DP - 1)]
     pltpu.make_async_copy(others, others, g_recv).wait()
+
+    def block(m):
+        return gath.at[pl.ds(pl.multiple_of(m * DP, DP), DP)]
+
+    def relay(i):
+        return pltpu.make_async_remote_copy(
+            src_ref=block(mp), dst_ref=block(mp), send_sem=p_send.at[i], recv_sem=p_recv.at[mp],
+            device_id=(dp, lax.rem(mp + i, MP)), device_id_type=MESH,
+        )
+
+    for i in range(1, MP):
+        relay(i).start()
+    for i in range(1, MP):
+        m = lax.rem(mp + i, MP)
+        pltpu.make_async_copy(block(m), block(m), p_recv.at[m]).wait()
 
     RP = B * CP
     gf[...] = gath[...].astype(F32).reshape(MP, DP * RP, LANES)
@@ -184,17 +200,23 @@
     mine = jnp.sum(jnp.exp(logits), axis=1, keepdims=True)
     wide = sums.shape[2]
     diagonal = lax.broadcasted_iota(jnp.int32, (S, wide), 0) == lax.broadcasted_iota(jnp.int32, (S, wide), 1)
-    sums[me] = jnp.sum(jnp.where(diagonal, mine, 0.0), axis=0, keepdims=True)
-
-    @pl.loop(1, N)
+    sums[slot] = jnp.sum(jnp.where(diagonal, mine, 0.0), axis=0, keepdims=True)
+
+    def sum_send(i, m):
+        return pltpu.make_async_remote_copy(
+            src_ref=sums.at[slot], dst_ref=sums.at[slot], send_sem=s_send, recv_sem=s_recv,
+            device_id=(lax.rem(dp + i, DP), m), device_id_type=MESH,
+        )
+
+    @pl.loop(1, DP)
     def _(i):
-        p = lax.rem(me + i, N)
-        pltpu.make_async_remote_copy(
-            src_ref=sums.at[me], dst_ref=sums.at[me], send_sem=s_send, recv_sem=s_recv,
-            device_id=(p // MP, lax.rem(p, MP)), device_id_type=MESH,
-        ).start()
-
-    others_s = sums.at[pl.ds(0, N - 1)]
+        for j in range(MP):
+            sum_send(i, lax.rem(mp + j, MP)).start()
+
+    for j in range(1, MP):
+        sum_send(0, lax.rem(mp + j, MP)).start()
+
+    others_s = sums.at[pl.ds(0, DP * MP - 1)]
     pltpu.make_async_copy(others_s, others_s, s_recv).wait()
     everything = jnp.sum(sums[...], axis=0)
     log_total = jnp.log(jnp.sum(jnp.where(diagonal, everything, 0.0), axis=1, keepdims=True))
@@ -202,6 +224,7 @@
 
     for i in range(1, MP):
         head_send(i).wait_send()
+        relay(i).wait_send()
     pltpu.make_async_copy(others, others, g_send).wait()
     pltpu.make_async_copy(others_s, others_s, s_send).wait()
 
@@ -221,11 +244,10 @@
         dma = pltpu.SemaphoreType.DMA
         anywhere = pl.BlockSpec(memory_space=pl.ANY)
         vmem = pl.BlockSpec(memory_space=pltpu.VMEM)
-        smem = pl.BlockSpec(memory_space=pltpu.SMEM)
-        return pl.pallas_call(
+        hidden, log_probs = pl.pallas_call(
             functools.partial(kernel, DP, MP, B, H, HD, L, FW, CP),
-            out_shape=(jax.ShapeDtypeStruct((B, FW), BF16), jax.ShapeDtypeStruct((S, V), F32)),
-            in_specs=[smem] * 2 + [anywhere] * 11,
+            out_shape=(pltpu.VMEM((B, FW), BF16), pltpu.VMEM((S, V), F32)),
+            in_specs=[anywhere] * 13,
             out_specs=(vmem, vmem),
             scratch_shapes=[
                 pltpu.VMEM((B, H, HD), BF16),
@@ -239,13 +261,16 @@
                 pltpu.VMEM((pairs, HD, HD), F32),
                 pltpu.VMEM(out_weight.shape, BF16),
                 pltpu.VMEM((V, D), BF16),
+                pltpu.SMEM(lengths.shape, jnp.int32),
+                pltpu.SMEM(beta.shape, F32),
                 pltpu.VMEM((4, PP, HD), F32),
                 pltpu.VMEM((MP, PP, HD), BF16),
                 pltpu.VMEM((B * CP, LANES), F32),
                 pltpu.VMEM((N, B * CP, LANES), BF16),
                 pltpu.VMEM((MP, DP * B * CP, LANES), F32),
-                pltpu.VMEM((N, 1, up(S, LANES)), F32),
-                dma((6,)),
+                pltpu.VMEM((DP * MP, 1, up(S, LANES)), F32),
+                pltpu.VMEM((MP, 1, up(S, LANES)), F32),
+                dma((8,)),
                 dma((pairs,)),
                 dma((pairs,)),
                 dma((pairs,)),
@@ -257,6 +282,10 @@
                 dma,
                 dma,
                 dma,
+                dma((MP,)),
+                dma((MP,)),
+                dma((MP,)),
+                dma((MP,)),
             ],
             compiler_params=pltpu.CompilerParams(collective_id=0, has_side_effects=True),
             name="decode_step",
@@ -264,6 +293,7 @@
             lengths, beta, q_new, k_new, v_new, k_cache, v_cache, memory, norm_z, out_weight, residual_in,
             final_gain.reshape(1, D), embedding,
         )
+        return hidden, log_probs
 
     in_specs = (
         P("dp", "mp", None),

time: 28.8 us -> 25.1 us (0.87)
  Pallas kernels: 25.3 us -> 23 us
  local copies, waits for them, and re-layouts: 2.65 us -> 1.21 us
    pallas_call x1, Pallas kernels: 25.3 us -> 23 us  [body(): pl.pallas_call(functools.partial(kernel, DP, MP, B, H, HD, L, FW, CP), ou...]
    unnamed x2, local copies, waits for them, and re-layouts: 2.65 us -> 1.21 us
where the time goes in v2:
time: 25.1 us; the launch traced here: 24.9 us
  Pallas kernels  23 us (92%)
  local copies, waits for them, and re-layouts  1.21 us (5%)
  between operations  0.64 us (3%)
    pallas_call x1, Pallas kernels, body(): pl.pallas_call(functools.partial(kernel, DP, MP, B, H, HD, L, FW, CP), ou...  23 us
    unnamed x2, local copies, waits for them, and re-layouts  1.21 us

profile of v2, /device:TPU:0, one launch (start us, length us, event | category | flops | bytes accessed | tf_op | source)
XLA Modules:
  0.0 24.9 jit_solution(7943659086057797014)
XLA Ops:
  0.6 23.0 %decode_step.1 = (bf16[2,1024]{1,0:T(2,128)(2,1)S(1)}, f32[32,256]{1,0:T(8,128)S(1)}) custom-call(s32[2]{0:T(128)} %lengths_ref.1, f32[4]{0:T(128)} %beta_ref.1, bf16[2,4,256]{2,1,0:T(4,128)(2,1)} %q_hbm.1, bf16[2,4,256]{2,1,0:T(4,128)(2,1)} %kn_hbm.1, bf16[2,4,256]{2,1,0:T(4,128)(2,1)} %vn_hbm.1, bf16[2,4,1024,256]{3,2,1,0:T(8,128)(2,1)} %k_hbm.1, ...), custom_call_target="tpu_custom_call" | custom-call | tf_op jit(solution)/shard_map/decode_step/pallas_call | solution.py:247
  23.7 0.6 %copy.17 = bf16[2,1024]{1,0:T(2,128)(2,1)} copy(bf16[2,1024]{1,0:T(2,128)(2,1)S(1)} %get-tuple-element.2) | data formatting | bytes 8192
  24.3 0.6 %copy.18 = f32[32,256]{1,0:T(8,128)} copy(f32[32,256]{1,0:T(8,128)S(1)} %get-tuple-element.3) | data formatting | bytes 65536
